TPU v7x, 32 devices: a whole 2x2x4 slice. The times are simulated.
32 devices in a mesh: lat: 8 (over z, y), lon: 4 (over x, core).
Axes of the slice: x: 2, y: 2, z: 4, core: 2. Of those that a mesh axis runs over, the one named last changes fastest.
Arguments:
- predicted_state: bfloat16 [222, 320, 512], P(None, 'lat', 'lon'), may hold values from -30 to 30
- observed_state: bfloat16 [222, 320, 512], P(None, 'lat', 'lon'), may hold values from -30 to 30
- longterm_average_state: bfloat16 [222, 320, 512], P(None, 'lat', 'lon'), may hold values from -30 to 30
Outputs:
- blurred_mismatch_map: bfloat16 [222, 320, 512], P(None, 'lat', 'lon')
- quadratic_mean_mistake: float32 [222], replicated
- pattern_agreement: float32 [222], replicated
All inputs are finite; a program needn't handle non-finite values.
Results may differ from a plain program's by a relative error of at most 0.00155.
Values may be sent and summed in bfloat16 or wider, within the bound.
A program may use at most 128 MiB of HBM per device.

v0:
```python
import jax
import jax.numpy as jnp
from jax import lax
from jax.sharding import PartitionSpec as P

epsilon = 1e-06


def extended(cells, sides, width):
    for axis, dim in sides:
        count = lax.axis_size(axis)
        head = lax.slice_in_dim(cells, 0, width, axis=dim)
        tail = lax.slice_in_dim(cells, cells.shape[dim] - width, cells.shape[dim], axis=dim)
        cells = jnp.concatenate(
            [
                lax.ppermute(tail, axis, [(i, (i + 1) % count) for i in range(count)]),
                cells,
                lax.ppermute(head, axis, [((i + 1) % count, i) for i in range(count)]),
            ],
            axis=dim,
        )
    return cells


def deviation_from_normal(predicted_state, observed_state, longterm_average_state):
    normal_reference_state = longterm_average_state.astype(jnp.float32)
    return (
        predicted_state.astype(jnp.float32) - normal_reference_state,
        observed_state.astype(jnp.float32) - normal_reference_state,
    )


def vertical_sum(member):
    return member[:, :-2] + member[:, 1:-1] + member[:, 2:]


def horizontal_sum(member):
    return member[:, :, :-2] + member[:, :, 1:-1] + member[:, :, 2:]


def finish(running_accumulations, grid_cells):
    mean_fcst = running_accumulations[1] / grid_cells
    mean_true = running_accumulations[2] / grid_cells
    variance_fcst = running_accumulations[3] / grid_cells - mean_fcst * mean_fcst
    variance_true = running_accumulations[4] / grid_cells - mean_true * mean_true
    covariance = running_accumulations[5] / grid_cells - mean_fcst * mean_true
    quadratic_mean_mistake = jnp.sqrt(running_accumulations[0] / grid_cells)
    pattern_agreement = covariance / jnp.sqrt((variance_fcst + epsilon) * (variance_true + epsilon))
    return (quadratic_mean_mistake, pattern_agreement)


def local(predicted_state, observed_state, longterm_average_state):
    nearby_parallel_accumulated = predicted_state.shape[1]
    parallel_overall_accumulated = nearby_parallel_accumulated * lax.axis_size("lat")
    meridian_accumulated = predicted_state.shape[2] * lax.axis_size("lon")
    row_start = lax.axis_index("lat") * nearby_parallel_accumulated
    row_index = row_start + jnp.arange(nearby_parallel_accumulated, dtype=jnp.int32)
    stacked_inputs = jnp.stack([predicted_state, observed_state, longterm_average_state])
    rimmed = extended(stacked_inputs, (("lat", 2), ("lon", 3)), 1)
    widened = deviation_from_normal(rimmed[0], rimmed[1], rimmed[2])
    padded_index = row_start - 1 + jnp.arange(nearby_parallel_accumulated + 2, dtype=jnp.int32)
    inside = ((padded_index >= 0) & (padded_index < parallel_overall_accumulated)).astype(
        jnp.float32
    )[None, :, None]
    summed = tuple((horizontal_sum(vertical_sum(member * inside)) for member in widened))
    row_count = (
        3.0
        - (row_index == 0).astype(jnp.float32)
        - (row_index == parallel_overall_accumulated - 1).astype(jnp.float32)
    )
    divisor = (3.0 * row_count)[:, None]
    averaged_prediction = summed[0] / divisor
    averaged_observation = summed[1] / divisor
    prediction_mismatch = averaged_prediction - averaged_observation
    all_rows = jnp.arange(parallel_overall_accumulated, dtype=jnp.float32)
    cosine = jnp.cos(jnp.pi * (0.5 - all_rows / (parallel_overall_accumulated - 1)))
    weight_all = cosine / jnp.mean(cosine)
    cosine_factor_vector = lax.dynamic_slice_in_dim(
        weight_all, row_start, nearby_parallel_accumulated
    )[:, None]
    weighted_fcst = cosine_factor_vector * averaged_prediction
    weighted_true = cosine_factor_vector * averaged_observation
    running_accumulations = jnp.stack(
        [
            jnp.sum(cosine_factor_vector * prediction_mismatch * prediction_mismatch, axis=(1, 2)),
            jnp.sum(weighted_fcst, axis=(1, 2)),
            jnp.sum(weighted_true, axis=(1, 2)),
            jnp.sum(weighted_fcst * averaged_prediction, axis=(1, 2)),
            jnp.sum(weighted_true * averaged_observation, axis=(1, 2)),
            jnp.sum(weighted_fcst * averaged_observation, axis=(1, 2)),
        ]
    )
    totals = lax.psum(running_accumulations, ("lat", "lon"))
    quadratic_mean_mistake, pattern_agreement = finish(
        totals, float(parallel_overall_accumulated * meridian_accumulated)
    )
    return (prediction_mismatch.astype(jnp.bfloat16), quadratic_mean_mistake, pattern_agreement)


def solution(mesh):
    placed = (P(None, "lat", "lon"), P(None, "lat", "lon"), P(None, "lat", "lon"))
    return jax.shard_map(
        local,
        mesh=mesh,
        in_specs=placed,
        out_specs=(P(None, "lat", "lon"), P(), P()),
        check_vma=False,
    )
```

profile of v0, /device:TPU:0, one launch (start us, length us, event | category | flops | bytes accessed | tf_op | source)
XLA Modules:
  0.0 139.8 jit_solution(17298895487577244605)
XLA Ops:
  0.6 4.5 %copy.6 = bf16[222,40,128]{0,1,2:T(8,128)(2,1)S(1)} copy(bf16[222,40,128]{2,1,0:T(8,128)(2,1)} %param.3) | data formatting | bytes 4546560 | tf_op args[0]
  5.1 5.2 %copy.7 = bf16[222,40,128]{0,1,2:T(8,128)(2,1)} copy(bf16[222,40,128]{2,1,0:T(8,128)(2,1)} %param.4) | data formatting | bytes 4546560 | tf_op args[1]
  10.3 5.3 %copy.8 = bf16[222,40,128]{0,1,2:T(8,128)(2,1)} copy(bf16[222,40,128]{2,1,0:T(8,128)(2,1)} %param.5) | data formatting | bytes 4546560 | tf_op args[2]
  15.6 3.1 %pad_maximum_fusion.3 = (bf16[3,222,1,128]{1,2,3,0:T(2,128)(2,1)}, bf16[3,222,1,128]{1,2,3,0:T(2,128)(2,1)}) fusion(bf16[1,222,40,128]{1,2,3,0:T(8,128)(2,1)} %bitcast.25, bf16[1,222,40,128]{1,2,3,0:T(8,128)(2,1)} %bitcast.22, bf16[1,222,40,128]{1,2,3,0:T(8,128)(2,1)S(1)} %bitcast.19), kind=kLoop, calls=%fused_computation.30 | loop fusion | flops 1022976 | bytes 7160832 | tf_op jit(solution)/shard_map/slice | solution.py:13
  18.7 3.0 %collective-permute-start = (bf16[3,222,1,128]{1,2,3,0:T(2,128)(2,1)}, bf16[3,222,1,128]{1,2,3,0:T(2,128)(2,1)S(1)}, u32[]{:S(2)}, u32[]{:S(2)}) collective-permute-start(bf16[3,222,1,128]{1,2,3,0:T(2,128)(2,1)} %get-tuple-element.18), channel_id=1, source_target_pairs={{0,4},{4,8},{8,12},{12,16},{16,20},{20,24},{24,28},{28,0},{1,5},{5... | collective-permute-start | bytes 511496 | tf_op jit(solution)/shard_map/ppermute | solution.py:16
  21.7 3.0 %collective-permute-start.1 = (bf16[3,222,1,128]{1,2,3,0:T(2,128)(2,1)}, bf16[3,222,1,128]{1,2,3,0:T(2,128)(2,1)S(1)}, u32[]{:S(2)}, u32[]{:S(2)}) collective-permute-start(bf16[3,222,1,128]{1,2,3,0:T(2,128)(2,1)} %get-tuple-element.19), channel_id=1, source_target_pairs={{4,0},{8,4},{12,8},{16,12},{20,16},{24,20},{28,24},{0,28},{5,1},{9... | collective-permute-start | bytes 511496 | tf_op jit(solution)/shard_map/ppermute | solution.py:18
  24.8 0.7 fusion.11
  26.1 0.5 fusion.19
  26.6 0.6 fusion.10
  27.2 11.6 %collective-permute-done = bf16[3,222,1,128]{1,2,3,0:T(2,128)(2,1)S(1)} collective-permute-done((bf16[3,222,1,128]{1,2,3,0:T(2,128)(2,1)}, bf16[3,222,1,128]{1,2,3,0:T(2,128)(2,1)S(1)}, u32[]{:S(2)}, u32[]{:S(2)}) %collective-permute-start) | collective-permute-done | bytes 170528 | tf_op jit(solution)/shard_map/ppermute | solution.py:16
  38.8 2.1 %collective-permute-done.1 = bf16[3,222,1,128]{1,2,3,0:T(2,128)(2,1)S(1)} collective-permute-done((bf16[3,222,1,128]{1,2,3,0:T(2,128)(2,1)}, bf16[3,222,1,128]{1,2,3,0:T(2,128)(2,1)S(1)}, u32[]{:S(2)}, u32[]{:S(2)}) %collective-permute-start.1) | collective-permute-done | bytes 170528 | tf_op jit(solution)/shard_map/ppermute | solution.py:18
  40.9 1.5 %pad_maximum_fusion.8 = (bf16[3,222,42,1]{1,2,3,0:T(8,128)(2,1)}, bf16[3,222,42,1]{1,2,3,0:T(8,128)(2,1)}) fusion(bf16[3,222,1,128]{1,2,3,0:T(2,128)(2,1)S(1)} %collective-permute-done.1, bf16[3,222,1,128]{1,2,3,0:T(2,128)(2,1)S(1)} %collective-permute-done, bf16[1,222,40,128]{1,2,3,0:T(8,128)(2,1)} %bitcast.26, bf16[1,222,40,128]{1,2,3,0:T(8,128)(2,1)} %bitcast.23, ...), kind=kLoop, calls=%fused_computation.35 | loop fusion | flops 559440 | bytes 7272720 | tf_op jit(solution)/shard_map/slice | solution.py:13
  42.4 1.7 %collective-permute-start.3 = (bf16[3,222,42,1]{1,2,3,0:T(8,128)(2,1)}, bf16[3,222,42,1]{1,2,3,0:T(8,128)(2,1)S(1)}, u32[]{:S(2)}, u32[]{:S(2)}) collective-permute-start(bf16[3,222,42,1]{1,2,3,0:T(8,128)(2,1)} %get-tuple-element.17), channel_id=1, source_target_pairs={{1,0},{2,1},{3,2},{0,3},{5,4},{6,5},{7,6},{4,7},{9,8},{10,9},{11,1... | collective-permute-start | bytes 167840 | tf_op jit(solution)/shard_map/ppermute | solution.py:18
  44.2 0.5 and_convert_fusion
  44.7 0.7 dynamic_slice.3
  45.4 1.0 collective-permute-done.2
  46.5 10.1 %pad_maximum_fusion = bf16[3,222,42,130]{1,2,3,0:T(8,128)(2,1)S(1)} fusion(bf16[3,222,42,1]{1,2,3,0:T(8,128)(2,1)S(1)} %collective-permute-done.3, bf16[3,222,1,128]{1,2,3,0:T(2,128)(2,1)S(1)} %collective-permute-done.1, bf16[1,222,40,128]{1,2,3,0:T(8,128)(2,1)} %bitcast.27, bf16[1,222,40,128]{1,2,3,0:T(8,128)(2,1)} %bitcast.24, ...), kind=kLoop, calls=%fused_computation | loop fusion | flops 50909040 | bytes 14545440 | tf_op jit(solution)/shard_map/concatenate | solution.py:14
  56.6 5.5 %fusion.1 = (f32[222,42,130]{0,1,2:T(8,128)}, f32[222,42,130]{0,1,2:T(8,128)}) fusion(bf16[3,222,42,130]{1,2,3,0:T(8,128)(2,1)S(1)} %pad_maximum_fusion, f32[42]{0:T(128)S(1)} %copy-done.1), kind=kLoop, calls=%fused_computation.10 | loop fusion | flops 8484840 | bytes 16969848 | tf_op jit(solution)/shard_map/mul | solution.py:65
  62.1 16.3 %slice_add_fusion = (f32[222,40,130]{0,1,2:T(8,128)S(1)}, f32[222,40,130]{0,1,2:T(8,128)}) fusion(f32[222,42,130]{0,1,2:T(8,128)} %get-tuple-element.15, f32[222,42,130]{0,1,2:T(8,128)} %get-tuple-element.14), kind=kLoop, calls=%fused_computation.13 | loop fusion | flops 4617600 | bytes 36940800 | tf_op jit(solution)/shard_map/add | solution.py:34
  78.4 12.7 %fusion.5 = (f32[222]{0:T(256)S(1)}, f32[222]{0:T(256)S(1)}, f32[222]{0:T(256)S(1)}, f32[222]{0:T(256)S(1)}, f32[222]{0:T(256)S(1)}, /*index=5*/f32[222]{0:T(256...) fusion(f32[40]{0:T(128)S(1)} %dynamic_slice.3, f32[40]{0:T(128)S(1)} %copy-done, f32[222,40,130]{0,1,2:T(8,128)S(1)} %get-tuple-element.22, ...), kind=kLoop, calls=%fused_computation.18 | loop fusion | flops 22731468 | bytes 36378128 | tf_op jit(solution)/shard_map/reduce_sum | solution.py:90
  91.1 39.4 %psum.7 = f32[6,222]{1,0:T(8,128)S(1)} all-reduce(f32[6,222]{1,0:T(8,128)S(1)} %stack.43), channel_id=1, replica_groups=mesh['lat'=8,'lon'=4] {'lat','lon'}, use_global_device_ids=true, to_apply=%region_7.0 | all-reduce | flops 1332 | bytes 10656 | tf_op jit(solution)/shard_map/psum | solution.py:93
  130.5 0.6 fusion.15
  131.1 4.9 %subtract_convert_fusion = bf16[222,40,128]{0,1,2:T(8,128)(2,1)S(1)} fusion(f32[222,40,128]{0,1,2:T(8,128)} %get-tuple-element.13, f32[222,40,128]{0,1,2:T(8,128)} %get-tuple-element.12), kind=kLoop, calls=%fused_computation.27 | loop fusion | flops 2273280 | bytes 11366400 | tf_op jit(solution)/shard_map/convert_element_type | solution.py:97
  136.0 3.8 %copy.9 = bf16[222,40,128]{2,1,0:T(8,128)(2,1)} copy(bf16[222,40,128]{0,1,2:T(8,128)(2,1)S(1)} %subtract_convert_fusion) | data formatting | bytes 4546560
  (7 shorter events, 0.1 us)
Async XLA Ops:
  18.7 20.1 %collective-permute-start = (bf16[3,222,1,128]{1,2,3,0:T(2,128)(2,1)}, bf16[3,222,1,128]{1,2,3,0:T(2,128)(2,1)S(1)}, u32[]{:S(2)}, u32[]{:S(2)}) collective-permute-start(bf16[3,222,1,128]{1,2,3,0:T(2,128)(2,1)} %get-tuple-element.18), channel_id=1, source_target_pairs={{0,4},{4,8},{8,12},{12,16},{16,20},{20,24},{24,28},{28,0},{1,5},{5... | collective-permute-start | bytes 511496 | tf_op jit(solution)/shard_map/ppermute | solution.py:16
  21.7 19.2 %collective-permute-start.1 = (bf16[3,222,1,128]{1,2,3,0:T(2,128)(2,1)}, bf16[3,222,1,128]{1,2,3,0:T(2,128)(2,1)S(1)}, u32[]{:S(2)}, u32[]{:S(2)}) collective-permute-start(bf16[3,222,1,128]{1,2,3,0:T(2,128)(2,1)} %get-tuple-element.19), channel_id=1, source_target_pairs={{4,0},{8,4},{12,8},{16,12},{20,16},{24,20},{28,24},{0,28},{5,1},{9... | collective-permute-start | bytes 511496 | tf_op jit(solution)/shard_map/ppermute | solution.py:18
  42.4 4.0 %collective-permute-start.2 = (bf16[3,222,42,1]{1,2,3,0:T(8,128)(2,1)}, bf16[3,222,42,1]{1,2,3,0:T(8,128)(2,1)S(1)}, u32[]{:S(2)}, u32[]{:S(2)}) collective-permute-start(bf16[3,222,42,1]{1,2,3,0:T(8,128)(2,1)} %get-tuple-element.16), channel_id=1, source_target_pairs={{0,1},{1,2},{2,3},{3,0},{4,5},{5,6},{6,7},{7,4},{8,9},{9,10},{10,1... | collective-permute-start | bytes 167840 | tf_op jit(solution)/shard_map/ppermute | solution.py:16
  42.4 4.0 %collective-permute-start.3 = (bf16[3,222,42,1]{1,2,3,0:T(8,128)(2,1)}, bf16[3,222,42,1]{1,2,3,0:T(8,128)(2,1)S(1)}, u32[]{:S(2)}, u32[]{:S(2)}) collective-permute-start(bf16[3,222,42,1]{1,2,3,0:T(8,128)(2,1)} %get-tuple-element.17), channel_id=1, source_target_pairs={{1,0},{2,1},{3,2},{0,3},{5,4},{6,5},{7,6},{4,7},{9,8},{10,9},{11,1... | collective-permute-start | bytes 167840 | tf_op jit(solution)/shard_map/ppermute | solution.py:18
  45.4 11.1 %copy-start.1 = (f32[42]{0:T(128)S(1)}, f32[42]{0:T(128)}, u32[]{:S(2)}) copy-start(f32[42]{0:T(128)} %and_convert_fusion) | copy-start | bytes 508
  62.1 16.3 %copy-start = (f32[40]{0:T(128)S(1)}, f32[40]{0:T(128)}, u32[]{:S(2)}) copy-start(f32[40]{0:T(128)} %fusion.19) | copy-start | bytes 484
where the time goes:
time: 140 us
  other arithmetic  57 us (41%)
  blocking collectives  39.4 us (28%)
  local copies, waits for them, and re-layouts  19.5 us (14%)
  waiting for transfers between devices  14.7 us (10%)
  starting transfers between devices  7.78 us (6%)
    psum x1, blocking collectives, local(): totals = lax.psum(running_accumulations, ('lat', 'lon'))  39.4 us
    unnamed x8, local copies, waits for them, and re-layouts  18.7 us
    add x1, other arithmetic, vertical_sum(): return member[:, :-2] + member[:, 1:-1] + member[:, 2:]  16.3 us
    reduce_sum x1, other arithmetic, local(): jnp.sum(weighted_fcst * averaged_observation, axis=(1, 2))  12.7 us
    ppermute x2, waiting for transfers between devices, extended(): lax.ppermute(tail, axis, [(i, (i + 1) % count) for i in range(count)])  12.6 us
    concatenate x1, other arithmetic, extended(): jnp.concatenate([lax.ppermute(tail, axis, [(i, (i + 1) % count) for i in...  10.1 us
    mul x1, other arithmetic, local(): member * inside  5.51 us
    convert_element_type x1, other arithmetic, local(): prediction_mismatch.astype(jnp.bfloat16)  4.93 us
  transfers between devices with their start and end apart: 4, of which 4 were waited for; matrix products, arithmetic and copies ran while one was open for 2% of the time, Pallas kernels for 0%

commit v1 on v0

v1 whole, which is shorter than its diff:
```python
import functools

import jax
import jax.numpy as jnp
import numpy as np
from jax import lax
from jax.experimental import pallas as pl
from jax.experimental.pallas import tpu as pltpu
from jax.sharding import PartitionSpec as P

MESH = pl.DeviceIdType.MESH
LANES = 128
PAIRS = LANES // 2
epsilon = 1e-06


def lane_index(shape):
    return lax.broadcasted_iota(jnp.int32, shape, len(shape) - 1)


def around(axis, step, size):
    return lax.rem(lax.axis_index(axis) + (step + size), size)


def exchange_kernel(nlat, nlon, p_ref, o_ref, c_ref, g_ref, h_ref, tiles, q, ct, cb, rows, qr, cr, rr, send, recv):
    fields, height, width = p_ref.shape
    chunks = pl.cdiv(fields, PAIRS)
    blocks = width // LANES
    down, up = around("lat", 1, nlat), around("lat", -1, nlat)
    right, left = around("lon", 1, nlon), around("lon", -1, nlon)
    y, x = lax.axis_index("lat"), lax.axis_index("lon")
    routes = [
        (q, qr.at[0], (y, right)),
        (q, qr.at[1], (y, left)),
        (rows.at[1], rr.at[0], (down, x)),
        (rows.at[0], rr.at[1], (up, x)),
        (ct, cr.at[0], (down, right)),
        (ct, cr.at[1], (down, left)),
        (cb, cr.at[2], (up, right)),
        (cb, cr.at[3], (up, left)),
    ]
    barrier = pltpu.get_barrier_semaphore()
    for _, _, target in routes:
        pl.semaphore_signal(barrier, inc=1, device_id=target, device_id_type=MESH)

    lane = lane_index((height, LANES))
    for chunk in range(chunks):
        count = min(PAIRS, fields - chunk * PAIRS)

        def pack(j, totals):
            f = chunk * PAIRS + j
            keep = (lane >> 1) == j
            out = []
            for a, ref in enumerate((p_ref, o_ref, c_ref)):
                cells = ref[f].astype(jnp.float32)
                at = pl.multiple_of(f * 8, 8)
                for b in range(blocks):
                    cut = slice(b * LANES, (b + 1) * LANES)
                    tiles[0, a, b, pl.ds(at, 8), :] = cells[:8, cut]
                    tiles[1, a, b, pl.ds(at, 8), :] = cells[height - 8 :, cut]
                edge = cells
                if blocks > 1:
                    edge = jnp.where(lane == 0, cells[:, :LANES], cells[:, width - LANES :])
                out.append(jnp.where(keep, pltpu.roll(edge, 2 * j + 1, axis=1), totals[a]))
            return tuple(out)

        zero = jnp.zeros((height, LANES), jnp.float32)
        packed = lax.fori_loop(0, count, pack, (zero, zero, zero), unroll=2 if count % 2 == 0 else 1)
        for a in range(3):
            q[a, chunk] = packed[a].astype(jnp.bfloat16)
            ct[a, chunk] = packed[a][height - 8 :].astype(jnp.bfloat16)
            cb[a, chunk] = packed[a][:8].astype(jnp.bfloat16)
    for side, row in ((0, 0), (1, 7)):
        for a in range(3):
            for b in range(blocks):
                line = tiles[side, a, b, pl.ds(row, fields, stride=8), :]
                rows[side, a, pl.ds(0, fields), b * LANES : (b + 1) * LANES] = line.astype(jnp.bfloat16)

    pl.semaphore_wait(barrier, len(routes))
    copies = [
        pltpu.make_async_remote_copy(
            src_ref=src, dst_ref=dst, send_sem=send.at[i], recv_sem=recv.at[i], device_id=target, device_id_type=MESH
        )
        for i, (src, dst, target) in enumerate(routes)
    ]
    for copy in copies:
        copy.start()
    for copy in copies:
        copy.wait()

    inside = ((y > 0).astype(jnp.float32), (y < nlat - 1).astype(jnp.float32))

    def merged(west, east):
        shape = west[0].shape
        even = (lane_index(shape) & 1) == 0
        picked = [jnp.where(even, l.astype(jnp.float32), r.astype(jnp.float32)) for l, r in zip(west, east)]
        out = []
        for a in range(2):
            d = picked[a] - picked[2]
            out.append(jnp.where(even, pltpu.roll(d, LANES - 1, axis=1), pltpu.roll(d, 1, axis=1)))
        return out

    for chunk in range(chunks):
        mid = merged([qr[0, a, chunk] for a in range(3)], [qr[1, a, chunk] for a in range(3)])
        top = merged([cr[0, a, chunk] for a in range(3)], [cr[1, a, chunk] for a in range(3)])
        bottom = merged([cr[2, a, chunk] for a in range(3)], [cr[3, a, chunk] for a in range(3)])
        for a in range(2):
            g_ref[a, chunk, pl.ds(0, 8), :] = top[a] * inside[0]
            g_ref[a, chunk, pl.ds(8, height), :] = mid[a]
            g_ref[a, chunk, pl.ds(8 + height, 8), :] = bottom[a] * inside[1]
    wide = lane_index((fields, width))
    for side in range(2):
        line = [rr[side, a, pl.ds(0, fields), :].astype(jnp.float32) for a in range(3)]
        for a in range(2):
            d = line[a] - line[2]
            before = jnp.where(wide == 0, 0.0, pltpu.roll(d, 1, axis=1))
            after = jnp.where(wide == width - 1, 0.0, pltpu.roll(d, width - 1, axis=1))
            h_ref[a, side, pl.ds(0, fields), :] = (d + before + after) * inside[side]


def stencil_kernel(nlat, group, p_ref, o_ref, c_ref, g_ref, h_ref, m_ref, s_ref, hs, acc, wr):
    step = pl.program_id(0)
    block, height, width = p_ref.shape
    fields = block * pl.num_programs(0)
    blocks = width // LANES
    total_rows = nlat * height

    @pl.when(step == 0)
    def _():
        row = lax.axis_index("lat") * height + lax.broadcasted_iota(jnp.int32, (height, width), 0)
        spots = np.arange(total_rows, dtype=np.float64) / (total_rows - 1)
        mean = float(np.mean(np.cos(np.pi * (0.5 - spots))))
        place = row.astype(jnp.float32) / (total_rows - 1)
        wr[0] = jnp.cos(jnp.pi * (0.5 - place)) / mean
        count = 3.0 - (row == 0).astype(jnp.float32) - (row == total_rows - 1).astype(jnp.float32)
        wr[1] = 1.0 / (3.0 * count)

    lane = lane_index((height, width))
    first, last = lane == 0, lane == width - 1
    line = lane_index((1, width))
    ends = (line == 0) | (line == width - 1)

    def body(g, carry):
        weight, inverse = wr[0], wr[1]
        for u in range(group):
            local = g * group + u
            f = step * block + local
            chunk, j = f // PAIRS, lax.rem(f, PAIRS)
            normal = c_ref[local].astype(jnp.float32)
            smooth = []
            for a, ref in enumerate((p_ref, o_ref)):
                d = ref[local].astype(jnp.float32) - normal
                edge = pltpu.roll(g_ref[a, chunk], LANES - 1 - 2 * j, axis=1)
                if blocks > 1:
                    edge = jnp.concatenate([edge] * blocks, axis=1)
                mid = edge[8 : 8 + height]
                hs[u, a, 8 : 8 + height, :] = (
                    d
                    + jnp.where(first, mid, pltpu.roll(d, 1, axis=1))
                    + jnp.where(last, mid, pltpu.roll(d, width - 1, axis=1))
                )
                hs[u, a, 7:8, :] = h_ref[a, 0, pl.ds(f, 1), :] + jnp.where(ends, edge[7:8], 0.0)
                hs[u, a, 8 + height : 9 + height, :] = h_ref[a, 1, pl.ds(f, 1), :] + jnp.where(
                    ends, edge[8 + height : 9 + height], 0.0
                )
                box = hs[u, a, 7 : 7 + height, :] + hs[u, a, 8 : 8 + height, :] + hs[u, a, 9 : 9 + height, :]
                smooth.append(box * inverse)
            fcst, true = smooth
            gap = fcst - true
            m_ref[local] = gap.astype(jnp.bfloat16)
            wf, wt = weight * fcst, weight * true
            at = pl.multiple_of(f * 8, 8)
            for k, term in enumerate((weight * gap * gap, wf, wt, wf * fcst, wt * true, wf * true)):
                part = jnp.sum(term.reshape(height // 8, 8, width), axis=0)
                if blocks > 1:
                    part = sum(part[:, b * LANES : (b + 1) * LANES] for b in range(blocks))
                acc[k, pl.ds(at, 8), :] = part
        return carry

    lax.fori_loop(0, block // group, body, 0)

    @pl.when(step == pl.num_programs(0) - 1)
    def _():
        ones = jnp.ones((8, LANES), jnp.float32)
        count = acc.shape[1] // 8
        s_ref[...] = jnp.zeros_like(s_ref)
        for k in range(6):
            part = acc[k, pl.ds(0, count, stride=8), :]
            for s in range(1, 8):
                part = part + acc[k, pl.ds(s, count, stride=8), :]
            r = lax.dot_general(
                ones, part, (((1,), (1,)), ((), ())), precision=lax.Precision.HIGHEST, preferred_element_type=jnp.float32
            )
            s_ref[k : k + 1, pl.ds(0, count)] = r[:1]


def total_kernel(nlat, nlon, cells, s_ref, e_ref, a_ref, b1, b2, t1, send1, recv1, send2, recv2):
    y, x = lax.axis_index("lat"), lax.axis_index("lon")
    barrier = pltpu.get_barrier_semaphore()
    for d in range(1, nlon):
        pl.semaphore_signal(barrier, inc=1, device_id=(y, around("lon", d, nlon)), device_id_type=MESH)
    for d in range(1, nlat):
        pl.semaphore_signal(barrier, inc=1, device_id=(around("lat", d, nlat), x), device_id_type=MESH)
    pl.semaphore_wait(barrier, nlon - 1 + nlat - 1)

    def stage(src, buf, send, recv, axis, size, me):
        def copy(d, slot):
            peer = around(axis, d, size)
            target = (y, peer) if axis == "lon" else (peer, x)
            return pltpu.make_async_remote_copy(
                src_ref=src,
                dst_ref=buf.at[slot],
                send_sem=send.at[d],
                recv_sem=recv.at[slot],
                device_id=target,
                device_id_type=MESH,
            )

        for d in range(1, size):
            copy(d, me).start()
        buf[me] = src[...]
        for d in range(1, size):
            copy(d, around(axis, -d, size)).wait_recv()
        total = buf[0]
        for i in range(1, size):
            total = total + buf[i]
        for d in range(1, size):
            copy(d, me).wait_send()
        return total

    t1[...] = stage(s_ref, b1, send1, recv1, "lon", nlon, x)
    totals = stage(t1, b2, send2, recv2, "lat", nlat, y)
    n = e_ref.shape[1]
    part = [totals[k : k + 1, :n] / cells for k in range(6)]
    variance_fcst = part[3] - part[1] * part[1]
    variance_true = part[4] - part[2] * part[2]
    covariance = part[5] - part[1] * part[2]
    e_ref[...] = jnp.sqrt(part[0])
    a_ref[...] = covariance / jnp.sqrt((variance_fcst + epsilon) * (variance_true + epsilon))


def largest_divisor(n, limit):
    return max(d for d in range(1, limit + 1) if n % d == 0)


def local(nlat, nlon, p, o, c):
    fields, height, width = p.shape
    chunks = pl.cdiv(fields, PAIRS)
    blocks = width // LANES
    padded = pl.cdiv(fields, 16) * 16
    vmem = pl.BlockSpec(memory_space=pltpu.VMEM)
    bf16, f32 = jnp.bfloat16, jnp.float32
    g, h = pl.pallas_call(
        functools.partial(exchange_kernel, nlat, nlon),
        out_shape=(
            jax.ShapeDtypeStruct((2, chunks, height + 16, LANES), f32),
            jax.ShapeDtypeStruct((2, 2, padded, width), f32),
        ),
        in_specs=[vmem] * 3,
        out_specs=(vmem, vmem),
        scratch_shapes=[
            pltpu.VMEM((2, 3, blocks, fields * 8, LANES), f32),
            pltpu.VMEM((3, chunks, height, LANES), bf16),
            pltpu.VMEM((3, chunks, 8, LANES), bf16),
            pltpu.VMEM((3, chunks, 8, LANES), bf16),
            pltpu.VMEM((2, 3, padded, width), bf16),
            pltpu.VMEM((2, 3, chunks, height, LANES), bf16),
            pltpu.VMEM((4, 3, chunks, 8, LANES), bf16),
            pltpu.VMEM((2, 3, padded, width), bf16),
            pltpu.SemaphoreType.DMA((8,)),
            pltpu.SemaphoreType.DMA((8,)),
        ],
        compiler_params=pltpu.CompilerParams(collective_id=0, has_side_effects=True),
        name="exchange",
    )(p, o, c)

    block = largest_divisor(fields, 80)
    group = largest_divisor(block, 4)
    field_block = pl.BlockSpec((block, height, width), lambda i: (i, 0, 0))
    lanes_out = pl.cdiv(fields, LANES) * LANES
    m, s = pl.pallas_call(
        functools.partial(stencil_kernel, nlat, group),
        grid=(fields // block,),
        out_shape=(
            jax.ShapeDtypeStruct((fields, height, width), bf16),
            jax.ShapeDtypeStruct((8, lanes_out), f32),
        ),
        in_specs=[field_block] * 3 + [vmem] * 2,
        out_specs=(field_block, pl.BlockSpec((8, lanes_out), lambda i: (0, 0))),
        scratch_shapes=[
            pltpu.VMEM((group, 2, height + 16, width), f32),
            pltpu.VMEM((6, fields * 8, LANES), f32),
            pltpu.VMEM((2, height, width), f32),
        ],
        compiler_params=pltpu.CompilerParams(dimension_semantics=("arbitrary",)),
        name="stencil",
    )(p, o, c, g, h)

    e, a = pl.pallas_call(
        functools.partial(total_kernel, nlat, nlon, float(nlat * height * nlon * width)),
        out_shape=(jax.ShapeDtypeStruct((1, fields), f32), jax.ShapeDtypeStruct((1, fields), f32)),
        in_specs=[vmem],
        out_specs=(vmem, vmem),
        scratch_shapes=[
            pltpu.VMEM((nlon, 8, lanes_out), f32),
            pltpu.VMEM((nlat, 8, lanes_out), f32),
            pltpu.VMEM((8, lanes_out), f32),
            pltpu.SemaphoreType.DMA((nlon,)),
            pltpu.SemaphoreType.DMA((nlon,)),
            pltpu.SemaphoreType.DMA((nlat,)),
            pltpu.SemaphoreType.DMA((nlat,)),
        ],
        compiler_params=pltpu.CompilerParams(collective_id=1, has_side_effects=True),
        name="total",
    )(s)
    return m, e.reshape(fields), a.reshape(fields)


def solution(mesh):
    spec = P(None, "lat", "lon")
    return jax.shard_map(
        functools.partial(local, mesh.shape["lat"], mesh.shape["lon"]),
        mesh=mesh,
        in_specs=(spec, spec, spec),
        out_specs=(spec, P(), P()),
        check_vma=False,
    )
```

time: 140 us -> 66.1 us (0.47)
  Pallas kernels: 0 us -> 62.8 us
  other arithmetic: 57 us -> 0 us
  blocking collectives: 39.4 us -> 0 us
  local copies, waits for them, and re-layouts: 19.5 us -> 2.43 us
  waiting for transfers between devices: 14.7 us -> 0 us
  starting transfers between devices: 7.78 us -> 0 us
    pallas_call x0 -> x3, Pallas kernels: none -> 62.8 us  [the longest x1 27.1 us: local(): pl.pallas_call(functools.partial(exchange_kernel, nlat, nlon), out_shape=...]
    psum x1 -> x0, blocking collectives: 39.4 us -> none  [local(): totals = lax.psum(running_accumulations, ('lat', 'lon'))]
    add x1 -> x0, other arithmetic: 16.3 us -> none  [vertical_sum(): return member[:, :-2] + member[:, 1:-1] + member[:, 2:]]
    unnamed x8 -> x2, local copies, waits for them, and re-layouts: 18.7 us -> 2.43 us
    ppermute x4 -> x0, waiting for transfers between devices: 14.7 us -> none  [the longest x2 12.6 us: extended(): lax.ppermute(tail, axis, [(i, (i + 1) % count) for i in range(count)])]
    reduce_sum x2 -> x0, other arithmetic: 13.3 us -> none  [the longest x1 12.7 us: local(): jnp.sum(weighted_fcst * averaged_observation, axis=(1, 2))]
    concatenate x1 -> x0, other arithmetic: 10.1 us -> none  [extended(): jnp.concatenate([lax.ppermute(tail, axis, [(i, (i + 1) % count) for i in...]
    ppermute x4 -> x0, starting transfers between devices: 7.78 us -> none  [the longest x2 4.78 us: extended(): lax.ppermute(head, axis, [((i + 1) % count, i) for i in range(count)])]
  transfers between devices with their start and end apart: 4 -> 0, of which waited for: 4 -> 0; matrix products, arithmetic and copies ran while one was open for 2% -> 0% of each run, Pallas kernels for 0% -> 0%
where the time goes in v1:
time: 66.1 us; the launch traced here: 65.9 us
  Pallas kernels  62.8 us (95%)
  local copies, waits for them, and re-layouts  2.43 us (4%)
    pallas_call x1, Pallas kernels, local(): pl.pallas_call(functools.partial(exchange_kernel, nlat, nlon), out_shape=...  27.1 us
    pallas_call x1, Pallas kernels, local(): pl.pallas_call(functools.partial(stencil_kernel, nlat, group), grid=(fiel...  23.9 us
    pallas_call x1, Pallas kernels, local(): pl.pallas_call(functools.partial(total_kernel, nlat, nlon, float(nlat * h...  11.8 us
    unnamed x2, local copies, waits for them, and re-layouts  2.43 us

profile of v1, /device:TPU:0, one launch (start us, length us, event | category | flops | bytes accessed | tf_op | source)
XLA Modules:
  0.0 65.9 jit_solution(16299718236578073692)
XLA Ops:
  0.6 27.1 %exchange.1 = (f32[2,4,56,128]{3,2,1,0:T(8,128)}, f32[2,2,224,128]{3,2,1,0:T(8,128)}) custom-call(bf16[222,40,128]{2,1,0:T(8,128)(2,1)} %p_ref.3, bf16[222,40,128]{2,1,0:T(8,128)(2,1)} %o_ref.3, bf16[222,40,128]{2,1,0:T(8,128)(2,1)} %c_ref.3), custom_call_target="tpu_custom_call" | custom-call | tf_op jit(solution)/shard_map/exchange/pallas_call | solution.py:253
  27.7 23.9 %stencil.1 = (bf16[222,40,128]{2,1,0:T(8,128)(2,1)}, f32[8,256]{1,0:T(8,128)}) custom-call(bf16[222,40,128]{2,1,0:T(8,128)(2,1)} %p_ref.3, bf16[222,40,128]{2,1,0:T(8,128)(2,1)} %o_ref.3, bf16[222,40,128]{2,1,0:T(8,128)(2,1)} %c_ref.3, f32[2,4,56,128]{3,2,1,0:T(8,128)} %get-tuple-element.9.g_ref, f32[2,2,224,128]{3,2,1,0:T(8,128)} %get-tuple-element.10.h_ref), custom_call_target="tpu_custom_call" | custom-call | tf_op jit(solution)/shard_map/stencil/pallas_call | solution.py:281
  51.6 11.8 %total.1 = (f32[1,222]{1,0:T(1,128)}, f32[1,222]{1,0:T(1,128)}) custom-call(f32[8,256]{1,0:T(8,128)} %get-tuple-element.12.s_ref), custom_call_target="tpu_custom_call" | custom-call | tf_op jit(solution)/shard_map/total/pallas_call | solution.py:299
  63.5 1.2 %copy.8 = f32[222]{0:T(256)} copy(f32[222]{0:T(256)} %bitcast.3) | data formatting | bytes 1776
  64.7 1.2 %copy.9 = f32[222]{0:T(256)} copy(f32[222]{0:T(256)} %bitcast.2) | data formatting | bytes 1776

commit v2 on v0

v2 whole, which is shorter than its diff:
```python
import functools

import jax
import jax.numpy as jnp
import numpy as np
from jax import lax
from jax.experimental import pallas as pl
from jax.experimental.pallas import tpu as pltpu
from jax.sharding import PartitionSpec as P

MESH = pl.DeviceIdType.MESH
LANES = 128
PAIRS = LANES // 2
epsilon = 1e-06


def lane_index(shape):
    return lax.broadcasted_iota(jnp.int32, shape, len(shape) - 1)


def around(axis, step, size):
    return lax.rem(lax.axis_index(axis) + (step + size), size)


def plan(fields):
    group = max(d for d in range(1, 7) if fields % d == 0)
    groups = fields // group
    count = -(-groups // (PAIRS // group))
    sizes = [group * ((groups + i) // count) for i in range(count)]
    starts = [sum(sizes[:i]) for i in range(count)]
    return group, list(zip(starts, sizes))


def fused_kernel(
    nlat, nlon, p_hbm, o_hbm, c_hbm, m_hbm, out_ref,
    p_ref, o_ref, c_ref, m_ref, tiles, q, ct, cb, rows, qr, cr, rr, gb, hb, hs, acc, wr, sums, b1, t1, b2,
    load, store, send, recv, send1, recv1, send2, recv2,
):
    fields, height, width = p_ref.shape
    group, chunks = plan(fields)
    blocks = width // LANES
    down, up = around("lat", 1, nlat), around("lat", -1, nlat)
    right, left = around("lon", 1, nlon), around("lon", -1, nlon)
    y, x = lax.axis_index("lat"), lax.axis_index("lon")

    loads = []
    for k, (base, size) in enumerate(chunks):
        cut = pl.ds(base, size)
        loads.append(
            [
                pltpu.make_async_copy(src.at[cut], dst.at[cut], load.at[k, a])
                for a, (src, dst) in enumerate(((p_hbm, p_ref), (o_hbm, o_ref), (c_hbm, c_ref)))
            ]
        )
        for copy in loads[-1]:
            copy.start()

    barrier = pltpu.get_barrier_semaphore()
    greeted = [(y, around("lon", d, nlon)) for d in range(1, nlon)]
    greeted += [(around("lat", d, nlat), x) for d in range(1, nlat)]
    greeted += [(down, right), (down, left), (up, right), (up, left)]
    for target in greeted:
        pl.semaphore_signal(barrier, inc=1, device_id=target, device_id_type=MESH)

    def routes(k, size):
        used = pl.ds(0, -(-size // 16) * 16)
        pairs = [
            (rows.at[k, 1, :, used], rr.at[k, 0, :, used], (down, x)),
            (rows.at[k, 0, :, used], rr.at[k, 1, :, used], (up, x)),
            (q.at[k], qr.at[k, 0], (y, right)),
            (q.at[k], qr.at[k, 1], (y, left)),
            (ct.at[k], cr.at[k, 0], (down, right)),
            (ct.at[k], cr.at[k, 1], (down, left)),
            (cb.at[k], cr.at[k, 2], (up, right)),
            (cb.at[k], cr.at[k, 3], (up, left)),
        ]
        return [
            pltpu.make_async_remote_copy(
                src_ref=src,
                dst_ref=dst,
                send_sem=send.at[k, i],
                recv_sem=recv.at[k, i],
                device_id=target,
                device_id_type=MESH,
            )
            for i, (src, dst, target) in enumerate(pairs)
        ]

    lane = lane_index((height, LANES))
    copies = []
    for k, (base, size) in enumerate(chunks):
        for copy in loads[k]:
            copy.wait()

        def pack(j, totals):
            out = list(totals)
            for u in range(2 if size % 2 == 0 else 1):
                s = j * (2 if size % 2 == 0 else 1) + u
                keep = (lane >> 1) == s
                for a, ref in enumerate((p_ref, o_ref, c_ref)):
                    cells = ref[base + s].astype(jnp.float32)
                    at = pl.multiple_of(s * 8, 8)
                    for b in range(blocks):
                        cut = slice(b * LANES, (b + 1) * LANES)
                        tiles[0, a, b, pl.ds(at, 8), :] = cells[:8, cut]
                        tiles[1, a, b, pl.ds(at, 8), :] = cells[height - 8 :, cut]
                    edge = cells
                    if blocks > 1:
                        edge = jnp.where(lane == 0, cells[:, :LANES], cells[:, width - LANES :])
                    out[a] = jnp.where(keep, pltpu.roll(edge, 2 * s + 1, axis=1), out[a])
            return tuple(out)

        zero = jnp.zeros((height, LANES), jnp.float32)
        packed = lax.fori_loop(0, size // 2 if size % 2 == 0 else size, pack, (zero, zero, zero))
        for a in range(3):
            q[k, a] = packed[a].astype(jnp.bfloat16)
            ct[k, a] = packed[a][height - 8 :].astype(jnp.bfloat16)
            cb[k, a] = packed[a][:8].astype(jnp.bfloat16)
        for side, row in ((0, 0), (1, 7)):
            for a in range(3):
                for b in range(blocks):
                    line = tiles[side, a, b, pl.ds(row, PAIRS, stride=8), :]
                    rows[k, side, a, :, b * LANES : (b + 1) * LANES] = line.astype(jnp.bfloat16)
        if k == 0:
            pl.semaphore_wait(barrier, len(greeted))
        copies.append(routes(k, size))
        for copy in copies[k]:
            copy.start()

    total_rows = nlat * height
    row = y * height + lax.broadcasted_iota(jnp.int32, (height, width), 0)
    spots = np.arange(total_rows, dtype=np.float64) / (total_rows - 1)
    mean = float(np.mean(np.cos(np.pi * (0.5 - spots))))
    place = row.astype(jnp.float32) / (total_rows - 1)
    wr[0] = jnp.cos(jnp.pi * (0.5 - place)) / mean
    count = 3.0 - (row == 0).astype(jnp.float32) - (row == total_rows - 1).astype(jnp.float32)
    wr[1] = 1.0 / (3.0 * count)

    inside = ((y > 0).astype(jnp.float32), (y < nlat - 1).astype(jnp.float32))

    def merged(west, east):
        shape = west[0].shape
        even = (lane_index(shape) & 1) == 0
        picked = [jnp.where(even, l.astype(jnp.float32), r.astype(jnp.float32)) for l, r in zip(west, east)]
        out = []
        for a in range(2):
            d = picked[a] - picked[2]
            out.append(jnp.where(even, pltpu.roll(d, LANES - 1, axis=1), pltpu.roll(d, 1, axis=1)))
        return out

    wide = lane_index((PAIRS, width))
    full = lane_index((height, width))
    first, last = full == 0, full == width - 1
    thin = lane_index((1, width))
    ends = (thin == 0) | (thin == width - 1)
    stores = []
    for k, (base, size) in enumerate(chunks):
        for copy in copies[k]:
            copy.wait_recv()
        mid = merged([qr[k, 0, a] for a in range(3)], [qr[k, 1, a] for a in range(3)])
        top = merged([cr[k, 0, a] for a in range(3)], [cr[k, 1, a] for a in range(3)])
        bottom = merged([cr[k, 2, a] for a in range(3)], [cr[k, 3, a] for a in range(3)])
        for a in range(2):
            gb[a, 0:8, :] = top[a] * inside[0]
            gb[a, 8 : 8 + height, :] = mid[a]
            gb[a, 8 + height :, :] = bottom[a] * inside[1]
        for side in range(2):
            line = [rr[k, side, a].astype(jnp.float32) for a in range(3)]
            for a in range(2):
                d = line[a] - line[2]
                before = jnp.where(wide == 0, 0.0, pltpu.roll(d, 1, axis=1))
                after = jnp.where(wide == width - 1, 0.0, pltpu.roll(d, width - 1, axis=1))
                hb[a, side] = (d + before + after) * inside[side]

        def body(g, carry):
            for u in range(group):
                j = g * group + u
                normal = c_ref[base + j].astype(jnp.float32)
                for a, ref in enumerate((p_ref, o_ref)):
                    d = ref[base + j].astype(jnp.float32) - normal
                    edge = pltpu.roll(gb[a], LANES - 1 - 2 * j, axis=1)
                    if blocks > 1:
                        edge = jnp.concatenate([edge] * blocks, axis=1)
                    beside = edge[8 : 8 + height]
                    hs[u, a, 8 : 8 + height, :] = (
                        d
                        + jnp.where(first, beside, pltpu.roll(d, 1, axis=1))
                        + jnp.where(last, beside, pltpu.roll(d, width - 1, axis=1))
                    )
                    hs[u, a, 7:8, :] = hb[a, 0, pl.ds(j, 1), :] + jnp.where(ends, edge[7:8], 0.0)
                    hs[u, a, 8 + height : 9 + height, :] = hb[a, 1, pl.ds(j, 1), :] + jnp.where(
                        ends, edge[8 + height : 9 + height], 0.0
                    )
            for u in range(group):
                f = base + g * group + u
                totals = [None] * 6
                for t in range(0, height, 8):
                    weight, inverse = wr[0, t : t + 8], wr[1, t : t + 8]
                    fcst, true = [
                        (hs[u, a, 7 + t : 15 + t, :] + hs[u, a, 8 + t : 16 + t, :] + hs[u, a, 9 + t : 17 + t, :]) * inverse
                        for a in range(2)
                    ]
                    gap = fcst - true
                    m_ref[f, t : t + 8, :] = gap.astype(jnp.bfloat16)
                    wf, wt = weight * fcst, weight * true
                    for i, term in enumerate((weight * gap * gap, wf, wt, wf * fcst, wt * true, wf * true)):
                        totals[i] = term if totals[i] is None else totals[i] + term
                at = pl.multiple_of(f * 8, 8)
                for i in range(6):
                    part = totals[i]
                    if blocks > 1:
                        part = sum(part[:, b * LANES : (b + 1) * LANES] for b in range(blocks))
                    acc[i, pl.ds(at, 8), :] = part
            return carry

        lax.fori_loop(0, size // group, body, 0)
        cut = pl.ds(base, size)
        stores.append(pltpu.make_async_copy(m_ref.at[cut], m_hbm.at[cut], store.at[k]))
        stores[-1].start()

    ones = jnp.ones((8, 3 * LANES), jnp.bfloat16)
    sums[...] = jnp.zeros_like(sums)
    for i in range(6):
        part = acc[i, pl.ds(0, fields, stride=8), :]
        for s in range(1, 8):
            part = part + acc[i, pl.ds(s, fields, stride=8), :]
        pieces = []
        for _ in range(3):
            pieces.append(part.astype(jnp.bfloat16))
            part = part - pieces[-1].astype(jnp.float32)
        r = lax.dot_general(
            ones, jnp.concatenate(pieces, axis=1), (((1,), (1,)), ((), ())), preferred_element_type=jnp.float32
        )
        sums[i : i + 1, :fields] = r[:1]

    def stage(src, buf, send, recv, axis, size, me):
        def copy(d, slot):
            peer = around(axis, d, size)
            target = (y, peer) if axis == "lon" else (peer, x)
            return pltpu.make_async_remote_copy(
                src_ref=src,
                dst_ref=buf.at[slot],
                send_sem=send.at[d],
                recv_sem=recv.at[slot],
                device_id=target,
                device_id_type=MESH,
            )

        for d in range(1, size):
            copy(d, me).start()
        buf[me] = src[...]
        for d in range(1, size):
            copy(d, around(axis, -d, size)).wait_recv()
        total = buf[0]
        for i in range(1, size):
            total = total + buf[i]
        return total, lambda: [copy(d, me).wait_send() for d in range(1, size)]

    t1[...], sent1 = stage(sums, b1, send1, recv1, "lon", nlon, x)
    out_ref[...], sent2 = stage(t1, b2, send2, recv2, "lat", nlat, y)
    sent1()
    sent2()
    for chunk in copies:
        for copy in chunk:
            copy.wait_send()
    for copy in stores:
        copy.wait()


def finish(totals, cells):
    part = totals / cells
    variance_fcst = part[3] - part[1] * part[1]
    variance_true = part[4] - part[2] * part[2]
    covariance = part[5] - part[1] * part[2]
    return jnp.sqrt(part[0]), covariance / jnp.sqrt((variance_fcst + epsilon) * (variance_true + epsilon))


def local(nlat, nlon, p, o, c):
    fields, height, width = p.shape
    group, chunks = plan(fields)
    n = len(chunks)
    blocks = width // LANES
    lanes_out = pl.cdiv(fields, LANES) * LANES
    bf16, f32 = jnp.bfloat16, jnp.float32
    anywhere = pl.BlockSpec(memory_space=pl.ANY)
    m, s = pl.pallas_call(
        functools.partial(fused_kernel, nlat, nlon),
        out_shape=(
            jax.ShapeDtypeStruct((fields, height, width), bf16),
            jax.ShapeDtypeStruct((8, lanes_out), f32),
        ),
        in_specs=[anywhere] * 3,
        out_specs=(anywhere, pl.BlockSpec(memory_space=pltpu.VMEM)),
        scratch_shapes=[
            *[pltpu.VMEM((fields, height, width), bf16)] * 4,
            pltpu.VMEM((2, 3, blocks, PAIRS * 8, LANES), f32),
            pltpu.VMEM((n, 3, height, LANES), bf16),
            pltpu.VMEM((n, 3, 8, LANES), bf16),
            pltpu.VMEM((n, 3, 8, LANES), bf16),
            pltpu.VMEM((n, 2, 3, PAIRS, width), bf16),
            pltpu.VMEM((n, 2, 3, height, LANES), bf16),
            pltpu.VMEM((n, 4, 3, 8, LANES), bf16),
            pltpu.VMEM((n, 2, 3, PAIRS, width), bf16),
            pltpu.VMEM((2, height + 16, LANES), f32),
            pltpu.VMEM((2, 2, PAIRS, width), f32),
            pltpu.VMEM((group, 2, height + 16, width), f32),
            pltpu.VMEM((6, fields * 8, LANES), f32),
            pltpu.VMEM((2, height, width), f32),
            pltpu.VMEM((8, lanes_out), f32),
            pltpu.VMEM((nlon, 8, lanes_out), f32),
            pltpu.VMEM((8, lanes_out), f32),
            pltpu.VMEM((nlat, 8, lanes_out), f32),
            pltpu.SemaphoreType.DMA((n, 3)),
            pltpu.SemaphoreType.DMA((n,)),
            pltpu.SemaphoreType.DMA((n, 8)),
            pltpu.SemaphoreType.DMA((n, 8)),
            pltpu.SemaphoreType.DMA((nlon,)),
            pltpu.SemaphoreType.DMA((nlon,)),
            pltpu.SemaphoreType.DMA((nlat,)),
            pltpu.SemaphoreType.DMA((nlat,)),
        ],
        compiler_params=pltpu.CompilerParams(collective_id=0, has_side_effects=True),
        name="fused",
    )(p, o, c)
    e, a = finish(s[:, :fields], float(nlat * height * nlon * width))
    return m, e, a


def solution(mesh):
    spec = P(None, "lat", "lon")
    return jax.shard_map(
        functools.partial(local, mesh.shape["lat"], mesh.shape["lon"]),
        mesh=mesh,
        in_specs=(spec, spec, spec),
        out_specs=(spec, P(), P()),
        check_vma=False,
    )
```

time: 140 us -> 43.5 us (0.31)
  other arithmetic: 57 us -> 1.28 us
  blocking collectives: 39.4 us -> 0 us
  Pallas kernels: 0 us -> 38 us
  local copies, waits for them, and re-layouts: 19.5 us -> 3.41 us
  waiting for transfers between devices: 14.7 us -> 0 us
  starting transfers between devices: 7.78 us -> 0 us
    psum x1 -> x0, blocking collectives: 39.4 us -> none  [local(): totals = lax.psum(running_accumulations, ('lat', 'lon'))]
    pallas_call x0 -> x1, Pallas kernels: none -> 38 us  [local(): pl.pallas_call(functools.partial(fused_kernel, nlat, nlon), out_shape=(ja...]
    add x1 -> x0, other arithmetic: 16.3 us -> none  [vertical_sum(): return member[:, :-2] + member[:, 1:-1] + member[:, 2:]]
    unnamed x8 -> x1, local copies, waits for them, and re-layouts: 18.7 us -> 3.41 us
    ppermute x4 -> x0, waiting for transfers between devices: 14.7 us -> none  [the longest x2 12.6 us: extended(): lax.ppermute(tail, axis, [(i, (i + 1) % count) for i in range(count)])]
    reduce_sum x2 -> x0, other arithmetic: 13.3 us -> none  [the longest x1 12.7 us: local(): jnp.sum(weighted_fcst * averaged_observation, axis=(1, 2))]
    concatenate x1 -> x0, other arithmetic: 10.1 us -> none  [extended(): jnp.concatenate([lax.ppermute(tail, axis, [(i, (i + 1) % count) for i in...]
    ppermute x4 -> x0, starting transfers between devices: 7.78 us -> none  [the longest x2 4.78 us: extended(): lax.ppermute(head, axis, [((i + 1) % count, i) for i in range(count)])]
  transfers between devices with their start and end apart: 4 -> 0, of which waited for: 4 -> 0; matrix products, arithmetic and copies ran while one was open for 2% -> 0% of each run, Pallas kernels for 0% -> 0%
where the time goes in v2:
time: 43.5 us; the launch traced here: 43.3 us
  Pallas kernels  38 us (87%)
  local copies, waits for them, and re-layouts  3.41 us (8%)
  other arithmetic  1.28 us (3%)
  between operations  0.64 us (1%)
    pallas_call x1, Pallas kernels, local(): pl.pallas_call(functools.partial(fused_kernel, nlat, nlon), out_shape=(ja...  38 us
    unnamed x1, local copies, waits for them, and re-layouts  3.41 us

profile of v2, /device:TPU:0, one launch (start us, length us, event | category | flops | bytes accessed | tf_op | source)
XLA Modules:
  0.0 43.3 jit_solution(9313559156404345358)
XLA Ops:
  0.6 38.0 %fused.1 = (bf16[222,40,128]{2,1,0:T(8,128)(2,1)}, f32[8,256]{1,0:T(8,128)}) custom-call(bf16[222,40,128]{2,1,0:T(8,128)(2,1)} %p_hbm.1, bf16[222,40,128]{2,1,0:T(8,128)(2,1)} %o_hbm.1, bf16[222,40,128]{2,1,0:T(8,128)(2,1)} %c_hbm.1), custom_call_target="tpu_custom_call" | custom-call | tf_op jit(solution)/shard_map/fused/pallas_call | solution.py:286
  38.6 0.7 %slice_multiply_fusion = f32[8,222]{1,0:T(8,128)S(1)} fusion(f32[8,256]{1,0:T(8,128)} %get-tuple-element.6), kind=kLoop, calls=%fused_computation | loop fusion | flops 1776 | bytes 14208 | tf_op jit(solution)/shard_map/div | solution.py:271
  39.3 0.6 %fusion.3 = (f32[1,222]{1,0:T(1,128)}, f32[1,222]{1,0:T(1,128)}) fusion(f32[8,222]{1,0:T(8,128)S(1)} %slice_multiply_fusion), kind=kLoop, calls=%fused_computation.7 | loop fusion | flops 2220 | bytes 7104 | tf_op jit(solution)/shard_map/div | solution.py:275
  39.9 3.4 %copy.7 = bf16[222,40,128]{2,1,0:T(8,128)(2,1)} copy(bf16[222,40,128]{2,1,0:T(8,128)(2,1)} %get-tuple-element.12) | data formatting | bytes 4546560
